TPU v7x, 128 devices: a whole 4x4x4 slice. The times are simulated.
128 devices in a mesh: group: 4 (over y_hi, core), patch: 32 (over y_lo, x, z).
Axes of the slice: x: 4, y: 4 (y_hi: 2, y_lo: 2; y = y_hi * 2 + y_lo), z: 4, core: 2. Of those that a mesh axis runs over, the one named last changes fastest.
Arguments:
- fine_nodes: bfloat16 [131072, 512], P(('group', 'patch')), may hold values from -6 to 6
- coarse_nodes: bfloat16 [2048, 512], P(('group', 'patch')), may hold values from -6 to 6
- fine_edges: bfloat16 [524288, 512], P(('group', 'patch')), may hold values from -6 to 6
- fine_senders: int32 [524288], P(('group', 'patch')), may hold values from 0 to 1279
- fine_receivers: int32 [524288], P(('group', 'patch')), may hold values from 0 to 1023
- fine_live: int32 [128], P(('group', 'patch')), may hold values from 128 to 4096, as said below
- up_edges: bfloat16 [65536, 512], P(('group', 'patch')), may hold values from -6 to 6
- up_senders: int32 [65536], P(('group', 'patch')), may hold values from 0 to 1023
- up_receivers: int32 [65536], P(('group', 'patch')), may hold values from 0 to 2047
- down_edges: bfloat16 [65536, 512], P(('group', 'patch')), may hold values from -6 to 6
- down_senders: int32 [65536], P(('group', 'patch')), may hold values from 0 to 2047
- down_receivers: int32 [65536], P(('group', 'patch')), may hold values from 0 to 1023
- edge_in_weight: bfloat16 [1536, 512], replicated, may hold values from -0.15625 to 0.15625
- edge_in_bias: float32 [512], replicated, may hold values from -3 to 3
- edge_out_weight: bfloat16 [512, 512], replicated, may hold values from -0.25 to 0.25
- edge_out_bias: float32 [512], replicated, may hold values from -3 to 3
- edge_gain: float32 [512], replicated, may hold values from 0.25 to 1.75
- edge_shift: float32 [512], replicated, may hold values from -2 to 2
- node_in_weight: bfloat16 [1024, 512], replicated, may hold values from -0.1875 to 0.1875
- node_in_bias: float32 [512], replicated, may hold values from -3 to 3
- node_out_weight: bfloat16 [512, 512], replicated, may hold values from -0.25 to 0.25
- node_out_bias: float32 [512], replicated, may hold values from -3 to 3
- node_gain: float32 [512], replicated, may hold values from 0.25 to 1.75
- node_shift: float32 [512], replicated, may hold values from -2 to 2
Outputs:
- fine_out: bfloat16 [131072, 512], P(('group', 'patch'))
- coarse_out: bfloat16 [2048, 512], P(('group', 'patch'))
- fine_edges_out: bfloat16 [524288, 512], P(('group', 'patch'))
- up_edges_out: bfloat16 [65536, 512], P(('group', 'patch'))
- down_edges_out: bfloat16 [65536, 512], P(('group', 'patch'))
Inputs may be any that keep to these rules, and one draw needn't show every extreme that they name: `fine_live`: a multiple of 128; some patch has all 4096 slots live in every draw.
All inputs are finite; a program needn't handle non-finite values.
Results may differ from a plain program's by a relative error of at most 0.0049.
Values may be sent and summed in bfloat16 or wider, within the bound.
A program may use at most 128 MiB of HBM per device.

v0:
```python
import jax
import jax.numpy as jnp
from jax import lax
from jax.sharding import PartitionSpec as P

RIM = 128


def extended(shard, sides, width):
    for axis, dim in sides:
        size, length = (lax.axis_size(axis), shard.shape[dim])
        up = [(i, (i + 1) % size) for i in range(size)]
        down = [(j, i) for i, j in up]
        last = lax.slice_in_dim(shard, length - width, length, axis=dim)
        first = lax.slice_in_dim(shard, 0, width, axis=dim)
        before = lax.ppermute(last, axis, up)
        after = lax.ppermute(first, axis, down)
        shard = jnp.concatenate([before, shard, after], axis=dim)
    return shard


def split_up(shard, dim, size):
    lengths = shard.shape
    parts = shard.reshape(*lengths[:dim], size, lengths[dim] // size, *lengths[dim + 1 :])
    return jnp.moveaxis(parts, dim, 0)


def sent_and_summed(shard, axis, dim):
    size = lax.axis_size(axis)
    parts = lax.all_to_all(split_up(shard, dim, size), axis, 0, 0, tiled=True)
    return jnp.sum(parts, axis=0)


def perceptron(inputs, in_weight, in_bias, out_weight, out_bias, gain, shift):
    preact = jnp.dot(inputs, in_weight, preferred_element_type=jnp.float32) + in_bias
    hidden = jax.nn.silu(preact).astype(jnp.bfloat16)
    result = jnp.dot(hidden, out_weight, preferred_element_type=jnp.float32) + out_bias
    average = jnp.mean(result, axis=-1, keepdims=True)
    centred = result - average
    spread = jnp.mean(centred * centred, axis=-1, keepdims=True)
    return centred * lax.rsqrt(spread + 1e-05) * gain + shift


def body(
    fine_nodes,
    coarse_nodes,
    fine_edges,
    fine_senders,
    fine_receivers,
    fine_live,
    up_edges,
    up_senders,
    up_receivers,
    down_edges,
    down_senders,
    down_receivers,
    edge_in_weight,
    edge_in_bias,
    edge_out_weight,
    edge_out_bias,
    edge_gain,
    edge_shift,
    node_in_weight,
    node_in_bias,
    node_out_weight,
    node_out_bias,
    node_gain,
    node_shift,
):
    edge_params = (
        edge_in_weight,
        edge_in_bias,
        edge_out_weight,
        edge_out_bias,
        edge_gain,
        edge_shift,
    )
    node_params = (
        node_in_weight,
        node_in_bias,
        node_out_weight,
        node_out_bias,
        node_gain,
        node_shift,
    )
    node_count = fine_nodes.shape[0]
    fine_slots = fine_edges.shape[0]
    up_count = up_edges.shape[0]
    window = extended(fine_nodes, (("patch", 0),), RIM)
    gathered = lax.all_gather(coarse_nodes, ("group", "patch"), axis=0, tiled=True)
    coarse_count = gathered.shape[0]
    fine_in = jnp.concatenate(
        [fine_edges, window[fine_senders], fine_nodes[fine_receivers]], axis=1
    )
    up_in = jnp.concatenate([up_edges, fine_nodes[up_senders], gathered[up_receivers]], axis=1)
    down_in = jnp.concatenate(
        [down_edges, gathered[down_senders], fine_nodes[down_receivers]], axis=1
    )
    all_edges = jnp.concatenate([fine_edges, up_edges, down_edges], axis=0).astype(jnp.float32)
    updated = all_edges + perceptron(
        jnp.concatenate([fine_in, up_in, down_in], axis=0), *edge_params
    )
    live_mask = (jnp.arange(fine_slots) < fine_live[0])[:, None]
    fine_new = jnp.where(live_mask, updated[:fine_slots], all_edges[:fine_slots])
    up_new = updated[fine_slots : fine_slots + up_count]
    down_new = updated[fine_slots + up_count :]
    fine_sum = jax.ops.segment_sum(
        jnp.where(live_mask, fine_new, 0.0), fine_receivers, num_segments=node_count
    )
    fine_sum = (
        fine_sum + jax.ops.segment_sum(down_new, down_receivers, num_segments=node_count)
    ).astype(jnp.bfloat16)
    fine_out = fine_nodes.astype(jnp.float32) + perceptron(
        jnp.concatenate([fine_nodes, fine_sum], axis=1), *node_params
    )
    owned_count = coarse_nodes.shape[0]
    groups = lax.axis_size("group")
    patches = lax.axis_size("patch")
    partial_value = jax.ops.segment_sum(up_new, up_receivers, num_segments=coarse_count)
    partial_value = partial_value.reshape(groups, patches, owned_count, partial_value.shape[1])
    section_one = sent_and_summed(partial_value, "group", 0)
    coarse_total = sent_and_summed(section_one, "patch", 1).reshape(
        owned_count, partial_value.shape[3]
    )
    coarse_sum = coarse_total.astype(jnp.bfloat16)
    coarse_out = coarse_nodes.astype(jnp.float32) + perceptron(
        jnp.concatenate([coarse_nodes, coarse_sum], axis=1), *node_params
    )
    return (
        fine_out.astype(jnp.bfloat16),
        coarse_out.astype(jnp.bfloat16),
        fine_new.astype(jnp.bfloat16),
        up_new.astype(jnp.bfloat16),
        down_new.astype(jnp.bfloat16),
    )


def solution(mesh):
    return jax.shard_map(
        body,
        mesh=mesh,
        in_specs=(
            P(("group", "patch"), None),
            P(("group", "patch"), None),
            P(("group", "patch"), None),
            P(("group", "patch")),
            P(("group", "patch")),
            P(("group", "patch")),
            P(("group", "patch"), None),
            P(("group", "patch")),
            P(("group", "patch")),
            P(("group", "patch"), None),
            P(("group", "patch")),
            P(("group", "patch")),
            P(),
            P(),
            P(),
            P(),
            P(),
            P(),
            P(),
            P(),
            P(),
            P(),
            P(),
            P(),
        ),
        out_specs=(
            P(("group", "patch"), None),
            P(("group", "patch"), None),
            P(("group", "patch"), None),
            P(("group", "patch"), None),
            P(("group", "patch"), None),
        ),
        check_vma=False,
    )
```

profile of v0, /device:TPU:1, one launch (start us, length us, event | category | flops | bytes accessed | tf_op | source)
XLA Modules:
  0.0 490.3 jit_solution(15975151159262812078)
XLA Ops:
  9.5 2.5 collective-permute-start
  12.0 5.3 %collective-permute-start.1 = (bf16[128,512]{1,0:T(8,128)(2,1)S(1)}, bf16[128,512]{1,0:T(8,128)(2,1)S(1)}, u32[]{:S(2)}, u32[]{:S(2)}) collective-permute-start(bf16[128,512]{1,0:T(8,128)(2,1)S(1)} %get-tuple-element.25), channel_id=1, source_target_pairs={{1,0},{2,1},{3,2},{4,3},{5,4},{6,5},{7,6},{8,7},{9,8},{10,9},{11,1... | collective-permute-start | bytes 393224 | tf_op jit(solution)/shard_map/ppermute | solution.py:17
  18.6 2.0 copy.51
  20.7 6.4 %copy.49 = bf16[4096,512]{0,1:T(8,128)(2,1)} copy(bf16[4096,512]{1,0:T(8,128)(2,1)} %param.26) | data formatting | bytes 8388608 | tf_op args[2]
  29.5 6.6 %maximum_convert_fusion = f32[5120,512]{0,1:T(8,128)} fusion(bf16[512,512]{0,1:T(8,128)(2,1)} %copy.51, bf16[512,512]{0,1:T(8,128)(2,1)S(1)} %copy.50, bf16[4096,512]{0,1:T(8,128)(2,1)} %copy.49), kind=kLoop, calls=%fused_computation.32 | loop fusion | flops 15728640 | bytes 15728640 | tf_op jit(solution)/shard_map/convert_element_type | solution.py:99
  38.7 2.8 gather_fusion.5
  41.5 2.7 gather_fusion.2
  44.2 18.5 %gather_fusion.1 = bf16[4096,512]{1,0:T(8,128)(2,1)} fusion(bf16[1024,512]{1,0:T(8,128)(2,1)S(1)} %copy-done.2, s32[4096]{0:T(1024)} %fusion.49), kind=kCustom, calls=%fused_computation.1 | custom fusion | bytes 8404992 | tf_op jit(solution)/shard_map/gather | solution.py:93
  64.6 18.9 %gather_fusion = bf16[4096,512]{1,0:T(8,128)(2,1)} fusion(bf16[1280,512]{1,0:T(8,128)(2,1)} %pad_maximum_fusion, s32[4096]{0:T(1024)S(1)} %fusion.48), kind=kCustom, calls=%fused_computation | custom fusion | bytes 8404992 | tf_op jit(solution)/shard_map/gather | solution.py:93
  83.5 232.3 %all-gather.2.cloned.1.call-done = bf16[2048,512]{1,0:T(8,128)(2,1)} async-done(((bf16[16,512]{1,0:T(8,128)(2,1)}), bf16[2048,512]{1,0:T(8,128)(2,1)}) %all-gather.2.cloned.1.call-update) | async-done | bytes 2097168 | tf_op jit(solution)/shard_map/all_gather | solution.py:90
  315.8 4.5 gather_fusion.3
  320.3 4.5 gather_fusion.4
  324.9 27.5 %multiply_convert_fusion.clone.1.clone.4 = bf16[5120,512]{1,0:T(8,128)(2,1)} fusion(bf16[1536,512]{1,0:T(8,128)(2,1)S(1)} %copy-done, bf16[512,512]{1,0:T(8,128)(2,1)} %gather_fusion.5, bf16[512,512]{1,0:T(8,128)(2,1)} %gather_fusion.4, bf16[512,512]{1,0:T(8,128)(2,1)} %param.33, bf16[512,512]{1,0:T(8,128)(2,1)} %gather_fusion.3, ...), kind=kOutput, calls=%fused_computation.29.clone.clone.clone.clone.clone.1 | convolution fusion | flops 8210350080 | bytes 22546432 | tf_op jit(solution)/shard_map/dot_general | solution.py:35
  352.4 5.3 %add_reduce_fusion = (f32[5120]{0:T(1024)S(1)}, f32[5120,512]{0,1:T(8,128)S(1)}) fusion(f32[512]{0:T(512)S(1)} %copy-done.17, bf16[512,512]{1,0:T(8,128)(2,1)S(1)} %copy-done.25, bf16[5120,512]{1,0:T(8,128)(2,1)} %multiply_convert_fusion.clone.1.clone.4), kind=kOutput, calls=%fused_computation.30 | convolution fusion | flops 2689592320 | bytes 16275456 | tf_op jit(solution)/shard_map/dot_general | solution.py:37
  360.0 3.1 add_add_fusion
  363.1 3.8 copy-done.3
  368.0 2.5 copy.54
  370.5 6.5 %scatter_custom_fusion.2 = f32[2048,512]{1,0:T(8,128)} fusion(s32[512]{0:T(512)} %param.32, f32[512,512]{1,0:T(8,128)} %copy.54, f32[]{:T(128)} %constant.9.clone.1), kind=kCustom, calls=%fused_computation.40 | custom fusion | flops 262144 | bytes 4194816 | tf_op jit(solution)/shard_map/scatter-add | solution.py:119
  377.0 5.2 %all-to-all-start = ((f32[4,1,32,16,512]{4,3,2,1,0:T(8,128)}), f32[4,1,32,16,512]{4,3,2,1,0:T(8,128)}, u32[]{:S(2)}, u32[]{:S(2)}) async-start(f32[4,1,32,16,512]{4,3,2,1,0:T(8,128)} %bitcast.17), calls=%async_computation | async-start | bytes 8388608 | tf_op jit(solution)/shard_map/all_to_all | solution.py:30
  382.2 9.5 %broadcast_select_fusion = f32[4096,512]{0,1:T(8,128)} fusion(pred[4096]{0:T(1024)(128)(4,1)S(1)} %copy-done.9, f32[5120,512]{0,1:T(8,128)} %maximum_convert_fusion, f32[5120,512]{0,1:T(8,128)} %copy-done.3), kind=kLoop, calls=%fused_computation.34 | loop fusion | flops 4194304 | bytes 25169920 | tf_op jit(solution)/shard_map/jit(_where)/select_n | solution.py:108
  393.1 5.7 %scatter_custom_fusion.1 = f32[1024,512]{1,0:T(8,128)} fusion(s32[512]{0:T(512)} %param.35, f32[512,512]{1,0:T(8,128)} %copy.53, f32[]{:T(128)} %constant.9.clone.1), kind=kCustom, calls=%fused_computation.53 | custom fusion | flops 262144 | bytes 2097664 | tf_op jit(solution)/shard_map/scatter-add | solution.py:111
  398.8 9.1 %copy.52 = f32[4096,512]{1,0:T(8,128)} copy(f32[4096,512]{0,1:T(8,128)} %broadcast_select_fusion) | data formatting | bytes 16777216 | tf_op jit(solution)/shard_map/jit(_where)/select_n | solution.py:108
  407.8 26.6 %scatter_custom_fusion = f32[1024,512]{1,0:T(8,128)} fusion(s32[4096]{0:T(1024)} %param.28, f32[4096,512]{1,0:T(8,128)} %copy.52, f32[]{:T(128)} %constant.9.clone.1), kind=kCustom, calls=%fused_computation.55 | custom fusion | flops 2097152 | bytes 2097664 | tf_op jit(solution)/shard_map/scatter-add | solution.py:107
  434.5 2.6 add_convert_fusion.1
  437.1 4.6 add_reduce_fusion.1
  441.7 8.3 %fusion.23 = bf16[4096,512]{0,1:T(8,128)(2,1)} fusion(f32[5120,512]{0,1:T(8,128)} %maximum_convert_fusion, f32[5120,512]{0,1:T(8,128)} %copy-done.3, pred[4096]{0:T(1024)(128)(4,1)S(1)} %copy-done.9), kind=kLoop, calls=%fused_computation.35 | loop fusion | flops 2097152 | bytes 12587008 | tf_op jit(solution)/shard_map/convert_element_type | solution.py:132
  450.0 3.7 reduce_sum.76
  453.8 7.9 %all-to-all-start.1 = ((f32[32,1,1,16,512]{4,3,2,1,0:T(8,128)}), f32[32,1,1,16,512]{4,3,2,1,0:T(8,128)}, u32[]{:S(2)}, u32[]{:S(2)}) async-start(f32[32,1,1,16,512]{4,3,2,1,0:T(8,128)} %bitcast.3), calls=%async_computation.1 | async-start | bytes 2097152 | tf_op jit(solution)/shard_map/all_to_all | solution.py:30
  465.4 6.5 %copy.57 = bf16[4096,512]{1,0:T(8,128)(2,1)} copy(bf16[4096,512]{0,1:T(8,128)(2,1)} %fusion.23) | data formatting | bytes 8388608
  471.9 1.9 multiply_reduce_fusion.1
  473.9 3.3 add_convert_fusion
  477.2 2.3 copy.56
  (90 shorter events, 22.3 us)
Async XLA Ops:
  7.2 317.7 %copy-start = (bf16[1536,512]{1,0:T(8,128)(2,1)S(1)}, bf16[1536,512]{1,0:T(8,128)(2,1)}, u32[]{:S(2)}) copy-start(bf16[1536,512]{1,0:T(8,128)(2,1)} %param.36) | copy-start | bytes 4718596
  7.2 308.6 %all-gather.2.cloned.1.call-start = ((), (), s32[]{:S(2)}) async-start(), calls=%async_computation.2 | async-start | bytes 2113536 | tf_op jit(solution)/shard_map/all_gather | solution.py:90
  9.5 53.8 %collective-permute-start = (bf16[128,512]{1,0:T(8,128)(2,1)}, bf16[128,512]{1,0:T(8,128)(2,1)S(1)}, u32[]{:S(2)}, u32[]{:S(2)}) collective-permute-start(bf16[128,512]{1,0:T(8,128)(2,1)} %get-tuple-element.24), channel_id=1, source_target_pairs={{0,1},{1,2},{2,3},{3,4},{4,5},{5,6},{6,7},{7,8},{8,9},{9,10},{10,1... | collective-permute-start | bytes 393224 | tf_op jit(solution)/shard_map/ppermute | solution.py:16
  12.0 51.3 %collective-permute-start.1 = (bf16[128,512]{1,0:T(8,128)(2,1)S(1)}, bf16[128,512]{1,0:T(8,128)(2,1)S(1)}, u32[]{:S(2)}, u32[]{:S(2)}) collective-permute-start(bf16[128,512]{1,0:T(8,128)(2,1)S(1)} %get-tuple-element.25), channel_id=1, source_target_pairs={{1,0},{2,1},{3,2},{4,3},{5,4},{6,5},{7,6},{8,7},{9,8},{10,9},{11,1... | collective-permute-start | bytes 393224 | tf_op jit(solution)/shard_map/ppermute | solution.py:17
  20.6 6.4 %copy-start.19 = (s32[512]{0:T(512)S(1)}, s32[512]{0:T(512)}, u32[]{:S(2)}) copy-start(s32[512]{0:T(512)} %param.31) | copy-start | bytes 6148
  20.6 7.0 %copy-start.20 = (s32[512]{0:T(512)S(1)}, s32[512]{0:T(512)}, u32[]{:S(2)}) copy-start(s32[512]{0:T(512)} %param.34) | copy-start | bytes 6148
  20.6 7.6 %copy-start.21 = (s32[512]{0:T(512)S(1)}, s32[512]{0:T(512)}, u32[]{:S(2)}) copy-start(s32[512]{0:T(512)} %param.32) | copy-start | bytes 6148
  20.6 8.2 %copy-start.22 = (s32[512]{0:T(512)S(1)}, s32[512]{0:T(512)}, u32[]{:S(2)}) copy-start(s32[512]{0:T(512)} %param.35) | copy-start | bytes 6148
  20.7 8.2 %copy-start.11 = (s32[4096]{0:T(1024)S(1)}, s32[4096]{0:T(1024)}, u32[]{:S(2)}) copy-start(s32[4096]{0:T(1024)} %param.27) | copy-start | bytes 49156
  20.7 8.2 %copy-start.12 = (s32[4096]{0:T(1024)S(1)}, s32[4096]{0:T(1024)}, u32[]{:S(2)}) copy-start(s32[4096]{0:T(1024)} %param.28) | copy-start | bytes 49156
  29.5 7.2 %copy-start.2 = (bf16[1024,512]{1,0:T(8,128)(2,1)S(1)}, bf16[1024,512]{1,0:T(8,128)(2,1)}, u32[]{:S(2)}) copy-start(bf16[1024,512]{1,0:T(8,128)(2,1)} %param.24) | copy-start | bytes 3145732
  64.6 251.2 %copy-start.14 = (s32[1024]{0:T(1024)S(1)}, s32[1024]{0:T(1024)}, u32[]{:S(2)}) copy-start(s32[1024]{0:T(1024)} %pad_clamp_fusion.2) | copy-start | bytes 12292
  83.4 236.9 %copy-start.13 = (s32[1024]{0:T(1024)S(1)}, s32[1024]{0:T(1024)}, u32[]{:S(2)}) copy-start(s32[1024]{0:T(1024)} %pad_clamp_fusion.1) | copy-start | bytes 12292
  83.5 241.4 %copy-start.26 = (f32[512]{0:T(512)S(1)}, f32[512]{0:T(512)}, u32[]{:S(2)}) copy-start(f32[512]{0:T(512)} %param.37) | copy-start | bytes 6148
  324.9 27.5 %copy-start.17 = (f32[512]{0:T(512)S(1)}, f32[512]{0:T(512)}, u32[]{:S(2)}) copy-start(f32[512]{0:T(512)} %param.39) | copy-start | bytes 6148
  324.9 27.5 %copy-start.25 = (bf16[512,512]{1,0:T(8,128)(2,1)S(1)}, bf16[512,512]{1,0:T(8,128)(2,1)}, u32[]{:S(2)}) copy-start(bf16[512,512]{1,0:T(8,128)(2,1)} %param.38) | copy-start | bytes 1572868
  357.7 2.2 copy-start.4
  357.7 2.3 copy-start.5
  357.7 2.3 copy-start.23
  357.7 2.3 copy-start.24
  363.1 3.8 copy-start.3
  377.0 5.2 %copy-start.9 = (pred[4096]{0:T(1024)(128)(4,1)S(1)}, pred[4096]{0:T(1024)(128)(4,1)}, u32[]{:S(2)}) copy-start(pred[4096]{0:T(1024)(128)(4,1)} %iota_compare_fusion) | copy-start | bytes 12292
  377.0 73.0 %all-to-all-start = ((f32[4,1,32,16,512]{4,3,2,1,0:T(8,128)}), f32[4,1,32,16,512]{4,3,2,1,0:T(8,128)}, u32[]{:S(2)}, u32[]{:S(2)}) async-start(f32[4,1,32,16,512]{4,3,2,1,0:T(8,128)} %bitcast.17), calls=%async_computation | async-start | bytes 8388608 | tf_op jit(solution)/shard_map/all_to_all | solution.py:30
  407.8 29.2 %copy-start.7 = (bf16[512,512]{1,0:T(8,128)(2,1)S(1)}, bf16[512,512]{1,0:T(8,128)(2,1)}, u32[]{:S(2)}) copy-start(bf16[512,512]{1,0:T(8,128)(2,1)} %param.44) | copy-start | bytes 1572868
  407.8 29.2 %copy-start.10 = (f32[512]{0:T(512)S(1)}, f32[512]{0:T(512)}, u32[]{:S(2)}) copy-start(f32[512]{0:T(512)} %param.45) | copy-start | bytes 6148
  407.8 29.2 %copy-start.18 = (f32[512]{0:T(512)S(1)}, f32[512]{0:T(512)}, u32[]{:S(2)}) copy-start(f32[512]{0:T(512)} %param.43) | copy-start | bytes 6148
  453.8 25.7 %all-to-all-start.1 = ((f32[32,1,1,16,512]{4,3,2,1,0:T(8,128)}), f32[32,1,1,16,512]{4,3,2,1,0:T(8,128)}, u32[]{:S(2)}, u32[]{:S(2)}) async-start(f32[32,1,1,16,512]{4,3,2,1,0:T(8,128)} %bitcast.3), calls=%async_computation.1 | async-start | bytes 2097152 | tf_op jit(solution)/shard_map/all_to_all | solution.py:30
  465.4 8.5 %copy-start.6 = (bf16[1024,512]{0,1:T(8,128)(2,1)S(1)}, bf16[1024,512]{0,1:T(8,128)(2,1)}, u32[]{:S(2)}) copy-start(bf16[1024,512]{0,1:T(8,128)(2,1)} %copy.48) | copy-start | bytes 3145732
  465.4 8.5 %copy-start.15 = (f32[512]{0:T(512)S(1)}, f32[512]{0:T(512)}, u32[]{:S(2)}) copy-start(f32[512]{0:T(512)} %param.47) | copy-start | bytes 6148
  465.4 8.5 %copy-start.16 = (f32[512]{0:T(512)S(1)}, f32[512]{0:T(512)}, u32[]{:S(2)}) copy-start(f32[512]{0:T(512)} %param.46) | copy-start | bytes 6148
  473.8 7.0 %copy-start.8 = (bf16[16,512]{1,0:T(8,128)(2,1)S(1)}, bf16[16,512]{1,0:T(8,128)(2,1)}, u32[]{:S(2)}) copy-start(bf16[16,512]{1,0:T(8,128)(2,1)} %param.25) | copy-start | bytes 49156
  473.8 9.6 %copy-start.1 = (bf16[1536,512]{1,0:T(8,128)(2,1)S(1)}, bf16[1536,512]{1,0:T(8,128)(2,1)}, u32[]{:S(2)}) copy-start(bf16[1536,512]{1,0:T(8,128)(2,1)} %param.36) | copy-start | bytes 4718596
Sparse Core Ops, SparseCore 0:
  9.7 306.0 all-gather.1
where the time goes:
time: 492 us; the launch traced here: 490 us
  waiting for transfers between devices  233 us (47%)
  local copies, waits for them, and re-layouts  95.4 us (19%)
  other arithmetic  86.8 us (18%)
  matrix products  39.1 us (8%)
  starting transfers between devices  20.9 us (4%)
  between operations  15 us (3%)
    all_gather x1, waiting for transfers between devices, body(): lax.all_gather(coarse_nodes, ('group', 'patch'), axis=0, tiled=True)  232 us
    dot_general x1, matrix products, perceptron(): jnp.dot(inputs, in_weight, preferred_element_type=jnp.float32) + in_bias  27.5 us
    scatter-add x1, other arithmetic, body(): jax.ops.segment_sum(jnp.where(live_mask, fine_new, 0.0), fine_receivers,...  26.6 us
    unnamed x62, local copies, waits for them, and re-layouts  26 us
    gather x1, local copies, waits for them, and re-layouts, body(): window[fine_senders]  18.9 us
    gather x1, local copies, waits for them, and re-layouts, body(): fine_nodes[fine_receivers]  18.5 us
    all_to_all x2, starting transfers between devices, sent_and_summed(): parts = lax.all_to_all(split_up(shard, dim, size), axis, 0, 0, tiled=True)  13 us
    dot_general x3, matrix products, perceptron(): jnp.dot(hidden, out_weight, preferred_element_type=jnp.float32) + out_bias  11.7 us
  transfers between devices with their start and end apart: 5, of which 1 were waited for; matrix products, arithmetic and copies ran while one was open for 31% of the time, Pallas kernels for 0%

commit v1 on v0

--- a/solution.py
+++ b/solution.py
@@ -87,7 +87,12 @@
     fine_slots = fine_edges.shape[0]
     up_count = up_edges.shape[0]
     window = extended(fine_nodes, (("patch", 0),), RIM)
-    gathered = lax.all_gather(coarse_nodes, ("group", "patch"), axis=0, tiled=True)
+    gathered = jnp.concatenate(
+        lax.all_to_all(
+            jnp.stack([coarse_nodes] * lax.axis_size(("group", "patch"))), ("group", "patch"), 0, 0
+        ),
+        axis=0,
+    )
     coarse_count = gathered.shape[0]
     fine_in = jnp.concatenate(
         [fine_edges, window[fine_senders], fine_nodes[fine_receivers]], axis=1

time: 492 us -> 254 us (0.52)
  waiting for transfers between devices: 233 us -> 0.01 us
  between operations: 15 us -> 1.66 us
  starting transfers between devices: 20.9 us -> 28 us
    all_gather x1 -> x0, waiting for transfers between devices: 232 us -> none  [body(): lax.all_gather(coarse_nodes, ('group', 'patch'), axis=0, tiled=True)]
    all_to_all x0 -> x1, starting transfers between devices: none -> 6.18 us  [body(): lax.all_to_all(jnp.stack([coarse_nodes] * lax.axis_size(('group', 'patch'...]
    unnamed x62 -> x66, local copies, waits for them, and re-layouts: 26 us -> 23.9 us
  transfers between devices with their start and end apart: 5 -> 5, of which waited for: 1 -> 0; matrix products, arithmetic and copies ran while one was open for 31% -> 60% of each run, Pallas kernels for 0% -> 0%
where the time goes in v1:
time: 254 us; the launch traced here: 252 us
  local copies, waits for them, and re-layouts  96 us (38%)
  other arithmetic  87 us (34%)
  matrix products  39.1 us (15%)
  starting transfers between devices  28 us (11%)
    dot_general x1, matrix products, perceptron(): jnp.dot(inputs, in_weight, preferred_element_type=jnp.float32) + in_bias  27.5 us
    scatter-add x1, other arithmetic, body(): jax.ops.segment_sum(jnp.where(live_mask, fine_new, 0.0), fine_receivers,...  26.6 us
    unnamed x66, local copies, waits for them, and re-layouts  23.9 us
    gather x1, local copies, waits for them, and re-layouts, body(): window[fine_senders]  19 us
    gather x1, local copies, waits for them, and re-layouts, body(): fine_nodes[fine_receivers]  18.6 us
    all_to_all x2, starting transfers between devices, sent_and_summed(): parts = lax.all_to_all(split_up(shard, dim, size), axis, 0, 0, tiled=True)  14 us
    dot_general x3, matrix products, perceptron(): jnp.dot(hidden, out_weight, preferred_element_type=jnp.float32) + out_bias  11.7 us
    select_n x1, other arithmetic, body(): jnp.where(live_mask, fine_new, 0.0)  9.46 us
  transfers between devices with their start and end apart: 5, of which 0 were waited for; matrix products, arithmetic and copies ran while one was open for 60% of the time, Pallas kernels for 0%

profile of v1, /device:TPU:1, one launch (start us, length us, event | category | flops | bytes accessed | tf_op | source)
XLA Modules:
  0.0 251.8 jit_solution(2462989248531562432)
XLA Ops:
  2.5 2.5 collective-permute-start
  5.0 5.3 %collective-permute-start.1 = (bf16[128,512]{1,0:T(8,128)(2,1)S(1)}, bf16[128,512]{1,0:T(8,128)(2,1)S(1)}, u32[]{:S(2)}, u32[]{:S(2)}) collective-permute-start(bf16[128,512]{1,0:T(8,128)(2,1)S(1)} %get-tuple-element.25), channel_id=1, source_target_pairs={{1,0},{2,1},{3,2},{4,3},{5,4},{6,5},{7,6},{8,7},{9,8},{10,9},{11,1... | collective-permute-start | bytes 393224 | tf_op jit(solution)/shard_map/ppermute | solution.py:17
  10.3 2.3 stack.2
  12.6 6.2 %all-to-all-start = ((bf16[128,16,512]{2,1,0:T(8,128)(2,1)}), bf16[128,16,512]{2,1,0:T(8,128)(2,1)}, u32[]{:S(2)}, u32[]{:S(2)}) async-start(bf16[128,16,512]{2,1,0:T(8,128)(2,1)} %stack.2), calls=%async_computation | async-start | bytes 4194304 | tf_op jit(solution)/shard_map/all_to_all | solution.py:91
  21.3 6.4 %copy.49 = bf16[4096,512]{0,1:T(8,128)(2,1)} copy(bf16[4096,512]{1,0:T(8,128)(2,1)} %param.26) | data formatting | bytes 8388608 | tf_op args[2]
  28.9 6.6 %maximum_convert_fusion = f32[5120,512]{0,1:T(8,128)} fusion(bf16[512,512]{0,1:T(8,128)(2,1)} %copy.51, bf16[512,512]{0,1:T(8,128)(2,1)S(1)} %copy.50, bf16[4096,512]{0,1:T(8,128)(2,1)} %copy.49), kind=kLoop, calls=%fused_computation.32 | loop fusion | flops 15728640 | bytes 15728640 | tf_op jit(solution)/shard_map/convert_element_type | solution.py:104
  38.0 2.8 %gather_fusion.5 = bf16[512,512]{1,0:T(8,128)(2,1)} fusion(bf16[1024,512]{1,0:T(8,128)(2,1)S(1)} %copy-done.2, s32[1024]{0:T(1024)} %pad_clamp_fusion), kind=kCustom, calls=%fused_computation.5 | custom fusion | bytes 1050624 | tf_op jit(solution)/shard_map/gather | solution.py:102
  40.8 2.8 %gather_fusion.2 = bf16[512,512]{1,0:T(8,128)(2,1)} fusion(bf16[1024,512]{1,0:T(8,128)(2,1)S(1)} %copy-done.2, s32[1024]{0:T(1024)} %pad_clamp_fusion.3), kind=kCustom, calls=%fused_computation.2 | custom fusion | bytes 1050624 | tf_op jit(solution)/shard_map/gather | solution.py:100
  43.6 18.6 %gather_fusion.1 = bf16[4096,512]{1,0:T(8,128)(2,1)} fusion(bf16[1024,512]{1,0:T(8,128)(2,1)S(1)} %copy-done.2, s32[4096]{0:T(1024)} %fusion.49), kind=kCustom, calls=%fused_computation.1 | custom fusion | bytes 8404992 | tf_op jit(solution)/shard_map/gather | solution.py:98
  64.0 19.0 %gather_fusion = bf16[4096,512]{1,0:T(8,128)(2,1)} fusion(bf16[1280,512]{1,0:T(8,128)(2,1)} %pad_maximum_fusion, s32[4096]{0:T(1024)S(1)} %fusion.48), kind=kCustom, calls=%fused_computation | custom fusion | bytes 8404992 | tf_op jit(solution)/shard_map/gather | solution.py:98
  83.0 4.5 %gather_fusion.4 = bf16[512,512]{1,0:T(8,128)(2,1)} fusion(bf16[2048,512]{1,0:T(8,128)(2,1)} %bitcast.1, s32[1024]{0:T(1024)S(1)} %copy-done.15), kind=kCustom, calls=%fused_computation.4 | custom fusion | bytes 1050624 | tf_op jit(solution)/shard_map/gather | solution.py:102
  87.6 4.5 %gather_fusion.3 = bf16[512,512]{1,0:T(8,128)(2,1)} fusion(bf16[2048,512]{1,0:T(8,128)(2,1)} %bitcast.1, s32[1024]{0:T(1024)S(1)} %copy-done.16), kind=kCustom, calls=%fused_computation.3 | custom fusion | bytes 1050624 | tf_op jit(solution)/shard_map/gather | solution.py:100
  92.1 27.5 %multiply_convert_fusion.clone.1.clone.4 = bf16[5120,512]{1,0:T(8,128)(2,1)} fusion(bf16[1536,512]{1,0:T(8,128)(2,1)S(1)} %copy-done, bf16[512,512]{1,0:T(8,128)(2,1)} %gather_fusion.5, bf16[512,512]{1,0:T(8,128)(2,1)} %gather_fusion.4, bf16[512,512]{1,0:T(8,128)(2,1)} %param.33, bf16[512,512]{1,0:T(8,128)(2,1)} %gather_fusion.3, ...), kind=kOutput, calls=%fused_computation.29.clone.clone.clone.clone.clone.1 | convolution fusion | flops 8210350080 | bytes 22546432 | tf_op jit(solution)/shard_map/dot_general | solution.py:35
  119.6 5.3 %add_reduce_fusion = (f32[5120]{0:T(1024)S(1)}, f32[5120,512]{0,1:T(8,128)S(1)}) fusion(f32[512]{0:T(512)S(1)} %copy-done.19, bf16[512,512]{1,0:T(8,128)(2,1)S(1)} %copy-done.27, bf16[5120,512]{1,0:T(8,128)(2,1)} %multiply_convert_fusion.clone.1.clone.4), kind=kOutput, calls=%fused_computation.30 | convolution fusion | flops 2689592320 | bytes 16275456 | tf_op jit(solution)/shard_map/dot_general | solution.py:37
  127.2 3.1 %add_add_fusion = f32[5120,512]{0,1:T(8,128)S(1)} fusion(f32[5120,512]{0,1:T(8,128)S(1)} %get-tuple-element.27, f32[512]{0:T(512)S(1)} %copy-done.25, f32[512]{0:T(512)S(1)} %copy-done.26, f32[5120]{0:T(1024)S(1)} %add_rsqrt_fusion, f32[5120]{0:T(1024)S(1)} %broadcast_multiply_fusion, f32[512]{0:T(512)S(1)} %copy-done.19, bf16[512,512]{0,1:T(8,128)(2,1)S(1)} %copy-done.5, ...), kind=kLoop, calls=%fused_computation.27 | loop fusion | flops 31457280 | bytes 26261504 | tf_op jit(solution)/shard_map/add | solution.py:105
  130.3 3.8 %copy-done.3 = f32[5120,512]{0,1:T(8,128)} copy-done((f32[5120,512]{0,1:T(8,128)}, f32[5120,512]{0,1:T(8,128)S(1)}, u32[]{:S(2)}) %copy-start.3) | copy-done | bytes 10485784
  135.3 2.5 %copy.54 = f32[512,512]{1,0:T(8,128)} copy(f32[512,512]{0,1:T(8,128)} %get-tuple-element.22) | data formatting | bytes 2097152 | tf_op jit(solution)/shard_map/slice | solution.py:110
  137.8 6.5 %scatter_custom_fusion.2 = f32[2048,512]{1,0:T(8,128)} fusion(s32[512]{0:T(512)} %param.32, f32[512,512]{1,0:T(8,128)} %copy.54, f32[]{:T(128)} %constant.9.clone.1), kind=kCustom, calls=%fused_computation.40 | custom fusion | flops 262144 | bytes 4194816 | tf_op jit(solution)/shard_map/scatter-add | solution.py:124
  144.3 6.1 %all-to-all-start.1 = ((f32[4,1,32,16,512]{4,3,2,1,0:T(8,128)}), f32[4,1,32,16,512]{4,3,2,1,0:T(8,128)}, u32[]{:S(2)}, u32[]{:S(2)}) async-start(f32[4,1,32,16,512]{4,3,2,1,0:T(8,128)} %bitcast.18), calls=%async_computation.1 | async-start | bytes 8388608 | tf_op jit(solution)/shard_map/all_to_all | solution.py:30
  150.3 9.5 %broadcast_select_fusion = f32[4096,512]{0,1:T(8,128)} fusion(pred[4096]{0:T(1024)(128)(4,1)S(1)} %copy-done.11, f32[5120,512]{0,1:T(8,128)} %maximum_convert_fusion, f32[5120,512]{0,1:T(8,128)} %copy-done.3), kind=kLoop, calls=%fused_computation.34 | loop fusion | flops 4194304 | bytes 25169920 | tf_op jit(solution)/shard_map/jit(_where)/select_n | solution.py:113
  161.2 5.7 %scatter_custom_fusion.1 = f32[1024,512]{1,0:T(8,128)} fusion(s32[512]{0:T(512)} %param.35, f32[512,512]{1,0:T(8,128)} %copy.53, f32[]{:T(128)} %constant.9.clone.1), kind=kCustom, calls=%fused_computation.53 | custom fusion | flops 262144 | bytes 2097664 | tf_op jit(solution)/shard_map/scatter-add | solution.py:116
  166.9 9.1 %copy.52 = f32[4096,512]{1,0:T(8,128)} copy(f32[4096,512]{0,1:T(8,128)} %broadcast_select_fusion) | data formatting | bytes 16777216 | tf_op jit(solution)/shard_map/jit(_where)/select_n | solution.py:113
  176.0 26.6 %scatter_custom_fusion = f32[1024,512]{1,0:T(8,128)} fusion(s32[4096]{0:T(1024)} %param.28, f32[4096,512]{1,0:T(8,128)} %copy.52, f32[]{:T(128)} %constant.9.clone.1), kind=kCustom, calls=%fused_computation.55 | custom fusion | flops 2097152 | bytes 2097664 | tf_op jit(solution)/shard_map/scatter-add | solution.py:112
  202.6 2.6 %add_convert_fusion.1 = bf16[1024,512]{1,0:T(8,128)(2,1)S(1)} fusion(f32[1024,512]{1,0:T(8,128)} %scatter_custom_fusion, f32[1024,512]{1,0:T(8,128)} %scatter_custom_fusion.1), kind=kLoop, calls=%fused_computation.45 | loop fusion | flops 1048576 | bytes 5242880 | tf_op jit(solution)/shard_map/convert_element_type | solution.py:117
  205.2 4.6 %add_reduce_fusion.1 = (f32[1024]{0:T(1024)S(1)}, f32[1024,512]{0,1:T(8,128)}) fusion(f32[512]{0:T(512)S(1)} %copy-done.12, bf16[512,512]{1,0:T(8,128)(2,1)S(1)} %copy-done.9, bf16[1024,512]{1,0:T(8,128)(2,1)} %param.42, bf16[1024,512]{1,0:T(8,128)(2,1)S(1)} %add_convert_fusion.1, bf16[1024,512]{1,0:T(8,128)(2,1)S(1)} %copy-done.2, f32[512]{0:T(512)S(1)} %copy-done.20), kind=kOutput, calls=%fused_computation.46 | convolution fusion | flops 1619000320 | bytes 5775360 | tf_op jit(solution)/shard_map/dot_general | solution.py:37
  209.9 8.5 %fusion.23 = bf16[4096,512]{0,1:T(8,128)(2,1)} fusion(f32[5120,512]{0,1:T(8,128)} %maximum_convert_fusion, f32[5120,512]{0,1:T(8,128)} %copy-done.3, pred[4096]{0:T(1024)(128)(4,1)S(1)} %copy-done.11), kind=kLoop, calls=%fused_computation.35 | loop fusion | flops 2097152 | bytes 12587008 | tf_op jit(solution)/shard_map/convert_element_type | solution.py:137
  218.3 3.8 %reduce_sum.76 = f32[32,16,512]{2,1,0:T(8,128)} reduce(f32[4,1,32,16,512]{4,3,2,1,0:T(8,128)} %all-to-all-done.1, f32[]{:T(128)} %constant.9.clone.1), dimensions={0,1}, to_apply=%region_7.8 | reduce | flops 786432 | bytes 5242884 | tf_op jit(solution)/shard_map/reduce_sum | solution.py:31
  222.1 8.0 %all-to-all-start.2 = ((f32[32,1,1,16,512]{4,3,2,1,0:T(8,128)}), f32[32,1,1,16,512]{4,3,2,1,0:T(8,128)}, u32[]{:S(2)}, u32[]{:S(2)}) async-start(f32[32,1,1,16,512]{4,3,2,1,0:T(8,128)} %bitcast.4), calls=%async_computation.2 | async-start | bytes 2097152 | tf_op jit(solution)/shard_map/all_to_all | solution.py:30
  233.7 6.5 %copy.57 = bf16[4096,512]{1,0:T(8,128)(2,1)} copy(bf16[4096,512]{0,1:T(8,128)(2,1)} %fusion.23) | data formatting | bytes 8388608
  240.2 1.9 multiply_reduce_fusion.1
  242.2 3.3 %add_convert_fusion = bf16[1024,512]{0,1:T(8,128)(2,1)} fusion(bf16[1024,512]{0,1:T(8,128)(2,1)S(1)} %copy-done.6, f32[1024,512]{0,1:T(8,128)} %get-tuple-element.29, f32[512]{0:T(512)S(1)} %copy-done.17, f32[512]{0:T(512)S(1)} %copy-done.18, f32[1024]{0:T(1024)S(1)} %add_rsqrt_fusion.1, f32[1024]{0:T(1024)S(1)} %broadcast_multiply_fusion.1, ...), kind=kLoop, calls=%fused_computation.42 | loop fusion | flops 4194304 | bytes 4208640 | tf_op jit(solution)/shard_map/convert_element_type | solution.py:135
  245.6 2.3 copy.56
  (94 shorter events, 21.7 us)
Async XLA Ops:
  0.6 91.5 %copy-start = (bf16[1536,512]{1,0:T(8,128)(2,1)S(1)}, bf16[1536,512]{1,0:T(8,128)(2,1)}, u32[]{:S(2)}) copy-start(bf16[1536,512]{1,0:T(8,128)(2,1)} %param.36) | copy-start | bytes 4718596
  0.6 18.1 %copy-start.21 = (s32[512]{0:T(512)S(1)}, s32[512]{0:T(512)}, u32[]{:S(2)}) copy-start(s32[512]{0:T(512)} %param.31) | copy-start | bytes 6148
  0.7 18.8 %copy-start.22 = (s32[512]{0:T(512)S(1)}, s32[512]{0:T(512)}, u32[]{:S(2)}) copy-start(s32[512]{0:T(512)} %param.34) | copy-start | bytes 6148
  0.7 19.4 %copy-start.23 = (s32[512]{0:T(512)S(1)}, s32[512]{0:T(512)}, u32[]{:S(2)}) copy-start(s32[512]{0:T(512)} %param.32) | copy-start | bytes 6148
  0.7 19.3 %copy-start.8 = (bf16[512,512]{1,0:T(8,128)(2,1)S(1)}, bf16[512,512]{1,0:T(8,128)(2,1)}, u32[]{:S(2)}) copy-start(bf16[512,512]{1,0:T(8,128)(2,1)} %param.30) | copy-start | bytes 1572868
  0.7 19.6 %copy-start.7 = (bf16[512,512]{1,0:T(8,128)(2,1)S(1)}, bf16[512,512]{1,0:T(8,128)(2,1)}, u32[]{:S(2)}) copy-start(bf16[512,512]{1,0:T(8,128)(2,1)} %param.33) | copy-start | bytes 1572868
  2.5 60.2 %collective-permute-start = (bf16[128,512]{1,0:T(8,128)(2,1)}, bf16[128,512]{1,0:T(8,128)(2,1)S(1)}, u32[]{:S(2)}, u32[]{:S(2)}) collective-permute-start(bf16[128,512]{1,0:T(8,128)(2,1)} %get-tuple-element.24), channel_id=1, source_target_pairs={{0,1},{1,2},{2,3},{3,4},{4,5},{5,6},{6,7},{7,8},{8,9},{9,10},{10,1... | collective-permute-start | bytes 393224 | tf_op jit(solution)/shard_map/ppermute | solution.py:16
  5.0 57.8 %collective-permute-start.1 = (bf16[128,512]{1,0:T(8,128)(2,1)S(1)}, bf16[128,512]{1,0:T(8,128)(2,1)S(1)}, u32[]{:S(2)}, u32[]{:S(2)}) collective-permute-start(bf16[128,512]{1,0:T(8,128)(2,1)S(1)} %get-tuple-element.25), channel_id=1, source_target_pairs={{1,0},{2,1},{3,2},{4,3},{5,4},{6,5},{7,6},{8,7},{9,8},{10,9},{11,1... | collective-permute-start | bytes 393224 | tf_op jit(solution)/shard_map/ppermute | solution.py:17
  12.6 70.4 %all-to-all-start = ((bf16[128,16,512]{2,1,0:T(8,128)(2,1)}), bf16[128,16,512]{2,1,0:T(8,128)(2,1)}, u32[]{:S(2)}, u32[]{:S(2)}) async-start(bf16[128,16,512]{2,1,0:T(8,128)(2,1)} %stack.2), calls=%async_computation | async-start | bytes 4194304 | tf_op jit(solution)/shard_map/all_to_all | solution.py:91
  21.3 7.0 %copy-start.24 = (s32[512]{0:T(512)S(1)}, s32[512]{0:T(512)}, u32[]{:S(2)}) copy-start(s32[512]{0:T(512)} %param.35) | copy-start | bytes 6148
  21.3 7.0 %copy-start.13 = (s32[4096]{0:T(1024)S(1)}, s32[4096]{0:T(1024)}, u32[]{:S(2)}) copy-start(s32[4096]{0:T(1024)} %param.27) | copy-start | bytes 49156
  21.3 7.0 %copy-start.14 = (s32[4096]{0:T(1024)S(1)}, s32[4096]{0:T(1024)}, u32[]{:S(2)}) copy-start(s32[4096]{0:T(1024)} %param.28) | copy-start | bytes 49156
  28.9 7.2 %copy-start.2 = (bf16[1024,512]{1,0:T(8,128)(2,1)S(1)}, bf16[1024,512]{1,0:T(8,128)(2,1)}, u32[]{:S(2)}) copy-start(bf16[1024,512]{1,0:T(8,128)(2,1)} %param.24) | copy-start | bytes 3145732
  64.0 19.0 %copy-start.15 = (s32[1024]{0:T(1024)S(1)}, s32[1024]{0:T(1024)}, u32[]{:S(2)}) copy-start(s32[1024]{0:T(1024)} %pad_clamp_fusion.1) | copy-start | bytes 12292
  83.0 4.6 %copy-start.16 = (s32[1024]{0:T(1024)S(1)}, s32[1024]{0:T(1024)}, u32[]{:S(2)}) copy-start(s32[1024]{0:T(1024)} %pad_clamp_fusion.2) | copy-start | bytes 12292
  83.0 9.1 %copy-start.28 = (f32[512]{0:T(512)S(1)}, f32[512]{0:T(512)}, u32[]{:S(2)}) copy-start(f32[512]{0:T(512)} %param.37) | copy-start | bytes 6148
  92.1 27.5 %copy-start.19 = (f32[512]{0:T(512)S(1)}, f32[512]{0:T(512)}, u32[]{:S(2)}) copy-start(f32[512]{0:T(512)} %param.39) | copy-start | bytes 6148
  92.1 27.5 %copy-start.27 = (bf16[512,512]{1,0:T(8,128)(2,1)S(1)}, bf16[512,512]{1,0:T(8,128)(2,1)}, u32[]{:S(2)}) copy-start(bf16[512,512]{1,0:T(8,128)(2,1)} %param.38) | copy-start | bytes 1572868
  124.9 2.3 copy-start.5
  124.9 2.3 copy-start.25
  130.3 3.8 %copy-start.3 = (f32[5120,512]{0,1:T(8,128)}, f32[5120,512]{0,1:T(8,128)S(1)}, u32[]{:S(2)}) copy-start(f32[5120,512]{0,1:T(8,128)S(1)} %add_add_fusion) | copy-start | bytes 31457284
  144.3 6.1 %copy-start.11 = (pred[4096]{0:T(1024)(128)(4,1)S(1)}, pred[4096]{0:T(1024)(128)(4,1)}, u32[]{:S(2)}) copy-start(pred[4096]{0:T(1024)(128)(4,1)} %iota_compare_fusion) | copy-start | bytes 12292
  144.3 74.1 %all-to-all-start.1 = ((f32[4,1,32,16,512]{4,3,2,1,0:T(8,128)}), f32[4,1,32,16,512]{4,3,2,1,0:T(8,128)}, u32[]{:S(2)}, u32[]{:S(2)}) async-start(f32[4,1,32,16,512]{4,3,2,1,0:T(8,128)} %bitcast.18), calls=%async_computation.1 | async-start | bytes 8388608 | tf_op jit(solution)/shard_map/all_to_all | solution.py:30
  176.0 29.2 %copy-start.9 = (bf16[512,512]{1,0:T(8,128)(2,1)S(1)}, bf16[512,512]{1,0:T(8,128)(2,1)}, u32[]{:S(2)}) copy-start(bf16[512,512]{1,0:T(8,128)(2,1)} %param.44) | copy-start | bytes 1572868
  176.0 29.2 %copy-start.12 = (f32[512]{0:T(512)S(1)}, f32[512]{0:T(512)}, u32[]{:S(2)}) copy-start(f32[512]{0:T(512)} %param.45) | copy-start | bytes 6148
  176.0 29.2 %copy-start.20 = (f32[512]{0:T(512)S(1)}, f32[512]{0:T(512)}, u32[]{:S(2)}) copy-start(f32[512]{0:T(512)} %param.43) | copy-start | bytes 6148
  222.1 25.8 %all-to-all-start.2 = ((f32[32,1,1,16,512]{4,3,2,1,0:T(8,128)}), f32[32,1,1,16,512]{4,3,2,1,0:T(8,128)}, u32[]{:S(2)}, u32[]{:S(2)}) async-start(f32[32,1,1,16,512]{4,3,2,1,0:T(8,128)} %bitcast.4), calls=%async_computation.2 | async-start | bytes 2097152 | tf_op jit(solution)/shard_map/all_to_all | solution.py:30
  233.7 8.5 %copy-start.6 = (bf16[1024,512]{0,1:T(8,128)(2,1)S(1)}, bf16[1024,512]{0,1:T(8,128)(2,1)}, u32[]{:S(2)}) copy-start(bf16[1024,512]{0,1:T(8,128)(2,1)} %copy.48) | copy-start | bytes 3145732
  233.7 8.5 %copy-start.17 = (f32[512]{0:T(512)S(1)}, f32[512]{0:T(512)}, u32[]{:S(2)}) copy-start(f32[512]{0:T(512)} %param.47) | copy-start | bytes 6148
  233.7 8.5 %copy-start.18 = (f32[512]{0:T(512)S(1)}, f32[512]{0:T(512)}, u32[]{:S(2)}) copy-start(f32[512]{0:T(512)} %param.46) | copy-start | bytes 6148
  242.2 7.0 %copy-start.10 = (bf16[16,512]{1,0:T(8,128)(2,1)S(1)}, bf16[16,512]{1,0:T(8,128)(2,1)}, u32[]{:S(2)}) copy-start(bf16[16,512]{1,0:T(8,128)(2,1)} %param.25) | copy-start | bytes 49156
  242.2 9.6 %copy-start.1 = (bf16[1536,512]{1,0:T(8,128)(2,1)S(1)}, bf16[1536,512]{1,0:T(8,128)(2,1)}, u32[]{:S(2)}) copy-start(bf16[1536,512]{1,0:T(8,128)(2,1)} %param.36) | copy-start | bytes 4718596
  (2 other events, 4.5 us)
